TPU v7x, 32 devices: a whole 2x2x4 slice. The times are simulated.
32 devices in a mesh: row: 4 (over y, x), col: 8 (over z, core).
Axes of the slice: x: 2, y: 2, z: 4, core: 2. Of those that a mesh axis runs over, the one named last changes fastest.
Arguments:
- operator: float32 [4096, 4096], P('row', 'col'), may hold values from -0.09375 to 0.09375
- state: float32 [4096, 4096], P('row', 'col'), may hold values from -60 to 60, as said below
- source: float32 [4096, 4096], P('row', 'col'), may hold values from -60 to 60, as said below
Outputs:
- state_next: float32 [4096, 4096], P('row', 'col')
- operator_fourth: float32 [4096, 4096], P('row', 'col')
Inputs may be any that keep to these rules, and one draw needn't show every extreme that they name: symmetric: state equals its transpose. symmetric: source equals its transpose.
All inputs are finite; a program needn't handle non-finite values.
Results may differ from a plain program's by a relative error of at most 0.000098.
Values sent between devices are 32-bit elements; how exact they have to be, the bound alone decides.
No kernel may reach another device: no remote copies, remote signals or barrier semaphores. Data moves between devices by JAX's collectives and lax.ppermute only.
A program may use at most 128 MiB of HBM per device.

v0:
```python
import jax
import jax.numpy as jnp
from jax import lax
from jax.sharding import PartitionSpec as P


def matmul(left, right):
    return jnp.dot(left, right, preferred_element_type=jnp.float32, precision=lax.Precision.HIGHEST)


def split_pieces(block, groups):
    rows, columns = block.shape
    width = columns // groups
    pieces = block.reshape(2, columns, groups, width).transpose(2, 0, 3, 1)
    return pieces.reshape(2 * groups, width, columns)


def join_pieces(pieces, groups):
    count, width, columns = pieces.shape
    joined = pieces.reshape(groups, 2, width, columns).transpose(1, 0, 2, 3)
    return joined.reshape(2 * groups * width, columns)


def folder(panel, piece):
    return matmul(panel, piece)


def on_device(operator, state, source):
    groups = lax.axis_size("row")
    row_panel = lax.all_gather(operator, "col", axis=1, tiled=True)
    product = matmul(row_panel, lax.all_gather(state, "row", axis=0, tiled=True))
    square = matmul(row_panel, lax.all_gather(operator, "row", axis=0, tiled=True))
    moved = lax.all_to_all(
        lax.all_to_all(
            split_pieces(product, groups), "row", split_axis=0, concat_axis=0, tiled=True
        ),
        "col",
        split_axis=0,
        concat_axis=0,
        tiled=True,
    )
    turned = join_pieces(
        lax.all_to_all(moved, "row", split_axis=0, concat_axis=0, tiled=True), groups
    )
    state_next = folder(row_panel, lax.all_gather(turned, "row", axis=0, tiled=True)) + source
    square_panel = lax.all_gather(square, "col", axis=1, tiled=True)
    operator_fourth = folder(square_panel, lax.all_gather(square, "row", axis=0, tiled=True))
    return (state_next, operator_fourth)


def solution(mesh):
    in_specs = (P("row", "col"), P("row", "col"), P("row", "col"))
    out_specs = (P("row", "col"), P("row", "col"))
    return jax.shard_map(
        on_device, mesh=mesh, in_specs=in_specs, out_specs=out_specs, check_vma=False
    )
```

profile of v0, /device:TPU:0, one launch (start us, length us, event | category | flops | bytes accessed | tf_op | source)
XLA Modules:
  0.0 784.8 jit_solution(5429908569219231628)
XLA Ops:
  7.2 0.7 all-gather.9.cloned.1.call-update
  7.9 0.7 all-gather.7.cloned.1.call-update
  8.7 0.7 all-gather.13.cloned.1.call-update
  9.4 0.0 all-gather.11.cloned.1.call-start
  9.4 90.6 %all-gather.9.cloned.1.call-done = f32[4096,512]{1,0:T(8,128)} async-done(((f32[1024,512]{1,0:T(8,128)}), f32[4096,512]{1,0:T(8,128)}) %all-gather.9.cloned.1.call-update) | async-done | bytes 8388624 | tf_op jit(solution)/shard_map/all_gather | solution.py:31
  100.1 152.7 %all-gather.7.cloned.1.call-done = f32[1024,4096]{1,0:T(8,128)} async-done(((f32[1024,512]{1,0:T(8,128)}), f32[1024,4096]{1,0:T(8,128)}) %all-gather.7.cloned.1.call-update) | async-done | bytes 16777232 | tf_op jit(solution)/shard_map/all_gather | solution.py:30
  252.8 31.0 %fusion = f32[1024,512]{1,0:T(8,128)} fusion(f32[1024,4096]{1,0:T(8,128)} %all-gather.7.cloned.1.call-done, f32[4096,512]{1,0:T(8,128)} %all-gather.9.cloned.1.call-done), kind=kOutput, calls=%fused_computation.1 | convolution fusion | flops 25769803776 | bytes 27262976 | tf_op jit(solution)/shard_map/dot_general | solution.py:8
  283.7 1.9 reshape.16
  285.7 1.8 copy.7
  287.5 51.3 %all_to_all.15 = f32[8,128,512]{2,1,0:T(8,128)S(1)} all-to-all(f32[8,128,512]{2,1,0:T(8,128)} %bitcast.18), channel_id=1, replica_groups=mesh['row'=4,'col'=8] {'row'}, dimensions={0} | all-to-all | bytes 4194304 | tf_op jit(solution)/shard_map/all_to_all | solution.py:34
  338.8 51.5 %all_to_all.16 = f32[8,128,512]{2,1,0:T(8,128)S(1)} all-to-all(f32[8,128,512]{2,1,0:T(8,128)S(1)} %all_to_all.15), channel_id=1, replica_groups=mesh['row'=4,'col'=8] {'col'}, dimensions={0} | all-to-all | bytes 4194304 | tf_op jit(solution)/shard_map/all_to_all | solution.py:33
  390.3 27.7 %all_to_all.17 = f32[8,128,512]{2,1,0:T(8,128)S(1)} all-to-all(f32[8,128,512]{2,1,0:T(8,128)S(1)} %all_to_all.16), channel_id=1, replica_groups=mesh['row'=4,'col'=8] {'row'}, dimensions={0} | all-to-all | bytes 4194304 | tf_op jit(solution)/shard_map/all_to_all | solution.py:43
  418.0 1.6 copy.8
  419.6 0.2 all-gather.17.cloned.1.call-start
  419.9 31.1 %fusion.1 = f32[1024,512]{1,0:T(8,128)} fusion(f32[1024,4096]{1,0:T(8,128)} %all-gather.7.cloned.1.call-done, f32[4096,512]{1,0:T(8,128)} %all-gather.13.cloned.1.call-done), kind=kOutput, calls=%fused_computation.2 | convolution fusion | flops 25769803776 | bytes 27262976 | tf_op jit(solution)/shard_map/dot_general | solution.py:8
  451.0 0.0 all-gather.15.cloned.1.call-start
  451.0 0.5 all-gather.15.cloned.1.call-update
  451.6 1.8 copy.9
  453.4 51.8 %all-gather.11.cloned.1.call-done = f32[4096,512]{1,0:T(8,128)} async-done(((f32[1024,512]{1,0:T(8,128)}), f32[4096,512]{1,0:T(8,128)}) %all-gather.11.cloned.1.call-update) | async-done | bytes 8388624 | tf_op jit(solution)/shard_map/all_gather | solution.py:45
  505.2 56.7 %bitcast_add_fusion = f32[1024,512]{0,1:T(8,128)S(1)} fusion(f32[1024,512]{0,1:T(8,128)} %copy.9, f32[4096,512]{1,0:T(8,128)} %all-gather.11.cloned.1.call-done, f32[1024,4096]{1,0:T(8,128)} %all-gather.7.cloned.1.call-done), kind=kOutput, calls=%fused_computation | convolution fusion | flops 25770328064 | bytes 29360128 | tf_op jit(solution)/shard_map/dot_general | solution.py:8
  562.0 1.8 copy.10
  563.8 30.6 %all-gather.17.cloned.1.call-done = f32[4096,512]{1,0:T(8,128)} async-done(((f32[1024,512]{1,0:T(8,128)}), f32[4096,512]{1,0:T(8,128)}) %all-gather.17.cloned.1.call-update) | async-done | bytes 8388624 | tf_op jit(solution)/shard_map/all_gather | solution.py:47
  594.4 152.6 %all-gather.15.cloned.1.call-done = f32[1024,4096]{1,0:T(8,128)} async-done(((f32[1024,512]{1,0:T(8,128)}), f32[1024,4096]{1,0:T(8,128)}) %all-gather.15.cloned.1.call-update) | async-done | bytes 16777232 | tf_op jit(solution)/shard_map/all_gather | solution.py:46
  747.0 31.0 %fusion.2 = f32[1024,512]{1,0:T(8,128)} fusion(f32[1024,4096]{1,0:T(8,128)} %all-gather.15.cloned.1.call-done, f32[4096,512]{1,0:T(8,128)} %all-gather.17.cloned.1.call-done), kind=kOutput, calls=%fused_computation.3 | convolution fusion | flops 25769803776 | bytes 27262976 | tf_op jit(solution)/shard_map/dot_general | solution.py:8
  (8 shorter events, 0.2 us)
Async XLA Ops:
  7.2 92.9 %all-gather.9.cloned.1.call-start = ((), (), s32[]{:S(2)}) async-start(), calls=%async_computation.4 | async-start | bytes 10485760 | tf_op jit(solution)/shard_map/all_gather | solution.py:31
  7.9 244.9 %all-gather.7.cloned.1.call-start = ((), (), s32[]{:S(2)}) async-start(), calls=%async_computation.3 | async-start | bytes 18874368 | tf_op jit(solution)/shard_map/all_gather | solution.py:30
  8.6 411.2 %all-gather.13.cloned.1.call-start = ((), (), s32[]{:S(2)}) async-start(), calls=%async_computation.6 | async-start | bytes 10485760 | tf_op jit(solution)/shard_map/all_gather | solution.py:32
  9.4 495.9 %all-gather.11.cloned.1.call-start = ((), (), s32[]{:S(2)}) async-start(), calls=%async_computation.5 | async-start | bytes 10485760 | tf_op jit(solution)/shard_map/all_gather | solution.py:45
  419.6 32.0 %copy-start = (f32[1024,512]{1,0:T(8,128)S(1)}, f32[1024,512]{1,0:T(8,128)}, u32[]{:S(2)}) copy-start(f32[1024,512]{1,0:T(8,128)} %param.5) | copy-start | bytes 6291460
  419.6 174.8 %all-gather.17.cloned.1.call-start = ((), (), s32[]{:S(2)}) async-start(), calls=%async_computation.8 | async-start | bytes 10485760 | tf_op jit(solution)/shard_map/all_gather | solution.py:47
  451.0 296.0 %all-gather.15.cloned.1.call-start = ((), (), s32[]{:S(2)}) async-start(), calls=%async_computation.7 | async-start | bytes 18874368 | tf_op jit(solution)/shard_map/all_gather | solution.py:46
Sparse Core Ops, SparseCore 0:
  9.8 90.1 all-gather.8
  101.7 151.0 all-gather.6
  254.6 107.1 all-gather.12
  419.7 85.4 all-gather.10
  506.9 87.4 all-gather.16
  595.9 151.0 all-gather.14
where the time goes:
time: 785 us
  waiting for transfers between devices  481 us (61%)
  matrix products  150 us (19%)
  blocking collectives  131 us (17%)
  between operations  14.2 us (2%)
  local copies, waits for them, and re-layouts  8.94 us (1%)
    all_gather x1, waiting for transfers between devices, on_device(): row_panel = lax.all_gather(operator, 'col', axis=1, tiled=True)  153 us
    all_gather x1, waiting for transfers between devices, on_device(): square_panel = lax.all_gather(square, 'col', axis=1, tiled=True)  153 us
    dot_general x4, matrix products, matmul(): jnp.dot(left, right, preferred_element_type=jnp.float32, precision=lax.Pr...  150 us
    all_gather x1, waiting for transfers between devices, on_device(): lax.all_gather(state, 'row', axis=0, tiled=True)  90.6 us
    all_gather x1, waiting for transfers between devices, on_device(): lax.all_gather(turned, 'row', axis=0, tiled=True)  51.8 us
    all_to_all x1, blocking collectives, on_device(): lax.all_to_all(lax.all_to_all(split_pieces(product, groups), 'row', split...  51.5 us
    all_to_all x1, blocking collectives, on_device(): lax.all_to_all(split_pieces(product, groups), 'row', split_axis=0, concat...  51.3 us
    all_gather x1, waiting for transfers between devices, on_device(): lax.all_gather(square, 'row', axis=0, tiled=True)  30.6 us
  transfers between devices with their start and end apart: 6, of which 5 were waited for; matrix products, arithmetic and copies ran while one was open for 16% of the time, Pallas kernels for 0%

commit v1 on v0

--- a/solution.py
+++ b/solution.py
@@ -27,7 +27,12 @@
 
 def on_device(operator, state, source):
     groups = lax.axis_size("row")
-    row_panel = lax.all_gather(operator, "col", axis=1, tiled=True)
+    ring = [operator]
+    for hop in range(7):
+        ring.append(lax.ppermute(ring[-1], "col", [(dev, (dev + 1) % 8) for dev in range(8)]))
+    row_panel = jnp.roll(
+        jnp.concatenate(ring[::-1], axis=1), (lax.axis_index("col") + 1) * ring[0].shape[1], axis=1
+    )
     product = matmul(row_panel, lax.all_gather(state, "row", axis=0, tiled=True))
     square = matmul(row_panel, lax.all_gather(operator, "row", axis=0, tiled=True))
     moved = lax.all_to_all(

time: 785 us -> 743 us (0.946)
  local copies, waits for them, and re-layouts: 8.94 us -> 47.9 us
  blocking collectives: 131 us -> 98.9 us
  matrix products: 150 us -> 124 us
  waiting for transfers between devices: 481 us -> 457 us
    ppermute x0 -> x7, waiting for transfers between devices: none -> 192 us  [on_device(): lax.ppermute(ring[-1], 'col', [(dev, (dev + 1) % 8) for dev in range(8)])]
    all_gather x1 -> x0, waiting for transfers between devices: 153 us -> none  [on_device(): row_panel = lax.all_gather(operator, 'col', axis=1, tiled=True)]
    all_gather x1, waiting for transfers between devices: 90.6 us -> 0.01 us  [on_device(): lax.all_gather(state, 'row', axis=0, tiled=True)]
    unnamed x4 -> x35, local copies, waits for them, and re-layouts: 3.63 us -> 41.1 us
    all_to_all x1, blocking collectives: 51.3 us -> 19.7 us  [on_device(): lax.all_to_all(split_pieces(product, groups), 'row', split_axis=0, concat...]
    all_gather x1, waiting for transfers between devices: 30.6 us -> 58 us  [on_device(): lax.all_gather(square, 'row', axis=0, tiled=True)]
    dot_general x4, matrix products: 150 us -> 124 us  [matmul(): jnp.dot(left, right, preferred_element_type=jnp.float32, precision=lax.Pr...]
  transfers between devices with their start and end apart: 6 -> 12, of which waited for: 5 -> 10; matrix products, arithmetic and copies ran while one was open for 16% -> 18% of each run, Pallas kernels for 0% -> 0%
where the time goes in v1:
time: 743 us
  waiting for transfers between devices  457 us (62%)
  matrix products  124 us (17%)
  blocking collectives  98.9 us (13%)
  local copies, waits for them, and re-layouts  47.9 us (6%)
  between operations  13.9 us (2%)
    ppermute x7, waiting for transfers between devices, on_device(): lax.ppermute(ring[-1], 'col', [(dev, (dev + 1) % 8) for dev in range(8)])  192 us
    all_gather x1, waiting for transfers between devices, on_device(): square_panel = lax.all_gather(square, 'col', axis=1, tiled=True)  153 us
    dot_general x4, matrix products, matmul(): jnp.dot(left, right, preferred_element_type=jnp.float32, precision=lax.Pr...  124 us
    all_gather x1, waiting for transfers between devices, on_device(): lax.all_gather(square, 'row', axis=0, tiled=True)  58 us
    all_gather x1, waiting for transfers between devices, on_device(): lax.all_gather(turned, 'row', axis=0, tiled=True)  53.6 us
    all_to_all x1, blocking collectives, on_device(): lax.all_to_all(lax.all_to_all(split_pieces(product, groups), 'row', split...  51.5 us
    unnamed x35, local copies, waits for them, and re-layouts  41.1 us
    all_to_all x1, blocking collectives, on_device(): lax.all_to_all(moved, 'row', split_axis=0, concat_axis=0, tiled=True)  27.7 us
  transfers between devices with their start and end apart: 12, of which 10 were waited for; matrix products, arithmetic and copies ran while one was open for 18% of the time, Pallas kernels for 0%

profile of v1, /device:TPU:0, one launch (start us, length us, event | category | flops | bytes accessed | tf_op | source)
XLA Modules:
  0.0 742.7 jit_solution(6406625914624660397)
XLA Ops:
  8.0 27.9 %collective-permute-done = f32[1024,512]{1,0:T(8,128)} collective-permute-done((f32[1024,512]{1,0:T(8,128)}, f32[1024,512]{1,0:T(8,128)}, u32[]{:S(2)}, u32[]{:S(2)}) %collective-permute-start) | collective-permute-done | bytes 2097184 | tf_op jit(solution)/shard_map/ppermute | solution.py:32
  35.8 27.5 %collective-permute-done.1 = f32[1024,512]{1,0:T(8,128)S(1)} collective-permute-done((f32[1024,512]{1,0:T(8,128)}, f32[1024,512]{1,0:T(8,128)S(1)}, u32[]{:S(2)}, u32[]{:S(2)}) %collective-permute-start.1) | collective-permute-done | bytes 2097184 | tf_op jit(solution)/shard_map/ppermute | solution.py:32
  64.7 27.3 %collective-permute-done.2 = f32[1024,512]{1,0:T(8,128)S(1)} collective-permute-done((f32[1024,512]{1,0:T(8,128)S(1)}, f32[1024,512]{1,0:T(8,128)S(1)}, u32[]{:S(2)}, u32[]{:S(2)}) %collective-permute-start.2) | collective-permute-done | bytes 2097184 | tf_op jit(solution)/shard_map/ppermute | solution.py:32
  93.3 27.3 %collective-permute-done.3 = f32[1024,512]{1,0:T(8,128)S(1)} collective-permute-done((f32[1024,512]{1,0:T(8,128)S(1)}, f32[1024,512]{1,0:T(8,128)S(1)}, u32[]{:S(2)}, u32[]{:S(2)}) %collective-permute-start.3) | collective-permute-done | bytes 2097184 | tf_op jit(solution)/shard_map/ppermute | solution.py:32
  121.9 27.3 %collective-permute-done.4 = f32[1024,512]{1,0:T(8,128)S(1)} collective-permute-done((f32[1024,512]{1,0:T(8,128)S(1)}, f32[1024,512]{1,0:T(8,128)S(1)}, u32[]{:S(2)}, u32[]{:S(2)}) %collective-permute-start.4) | collective-permute-done | bytes 2097184 | tf_op jit(solution)/shard_map/ppermute | solution.py:32
  150.4 27.4 %collective-permute-done.5 = f32[1024,512]{1,0:T(8,128)} collective-permute-done((f32[1024,512]{1,0:T(8,128)S(1)}, f32[1024,512]{1,0:T(8,128)}, u32[]{:S(2)}, u32[]{:S(2)}) %collective-permute-start.5) | collective-permute-done | bytes 2097184 | tf_op jit(solution)/shard_map/ppermute | solution.py:32
  177.9 27.5 %collective-permute-done.6 = f32[1024,512]{1,0:T(8,128)} collective-permute-done((f32[1024,512]{1,0:T(8,128)}, f32[1024,512]{1,0:T(8,128)}, u32[]{:S(2)}, u32[]{:S(2)}) %collective-permute-start.6) | collective-permute-done | bytes 2097184 | tf_op jit(solution)/shard_map/ppermute | solution.py:32
  205.4 3.1 constant_dynamic-update-slice_fusion.15
  208.4 3.1 constant_dynamic-update-slice_fusion.14
  211.5 3.2 constant_dynamic-update-slice_fusion.13
  214.7 3.2 constant_dynamic-update-slice_fusion.12
  221.0 3.6 constant_dynamic-update-slice_fusion.9
  226.1 3.1 constant_dynamic-update-slice_fusion.7
  238.1 3.1 constant_dynamic-update-slice_fusion.1
  242.7 31.0 %fusion.4 = f32[1024,512]{1,0:T(8,128)} fusion(f32[4096,512]{1,0:T(8,128)} %all-gather.6.cloned.1.call-done, f32[1024,8192]{1,0:T(8,128)} %constant_dynamic-update-slice_fusion, s32[]{:T(128)S(6)} %select_n.14), kind=kOutput, calls=%fused_computation.4 | convolution fusion | flops 25769803776 | bytes 27262980 | tf_op jit(solution)/shard_map/dot_general | solution.py:8
  277.4 19.7 %all_to_all.15 = f32[8,128,512]{2,1,0:T(8,128)S(1)} all-to-all(f32[8,128,512]{2,1,0:T(8,128)} %bitcast.13), channel_id=1, replica_groups=mesh['row'=4,'col'=8] {'row'}, dimensions={0} | all-to-all | bytes 4194304 | tf_op jit(solution)/shard_map/all_to_all | solution.py:39
  297.0 51.5 %all_to_all.16 = f32[8,128,512]{2,1,0:T(8,128)S(1)} all-to-all(f32[8,128,512]{2,1,0:T(8,128)S(1)} %all_to_all.15), channel_id=1, replica_groups=mesh['row'=4,'col'=8] {'col'}, dimensions={0} | all-to-all | bytes 4194304 | tf_op jit(solution)/shard_map/all_to_all | solution.py:38
  348.5 27.7 %all_to_all.17 = f32[8,128,512]{2,1,0:T(8,128)S(1)} all-to-all(f32[8,128,512]{2,1,0:T(8,128)S(1)} %all_to_all.16), channel_id=1, replica_groups=mesh['row'=4,'col'=8] {'row'}, dimensions={0} | all-to-all | bytes 4194304 | tf_op jit(solution)/shard_map/all_to_all | solution.py:48
  378.0 31.2 %fusion = f32[1024,512]{1,0:T(8,128)} fusion(f32[4096,512]{1,0:T(8,128)} %all-gather.10.cloned.1.call-done, f32[1024,8192]{1,0:T(8,128)} %constant_dynamic-update-slice_fusion, s32[]{:T(128)S(6)} %select_n.14), kind=kOutput, calls=%fused_computation | convolution fusion | flops 25769803776 | bytes 27262980 | tf_op jit(solution)/shard_map/dot_general | solution.py:8
  409.8 53.6 %all-gather.8.cloned.1.call-done = f32[4096,512]{1,0:T(8,128)} async-done(((f32[1024,512]{1,0:T(8,128)}), f32[4096,512]{1,0:T(8,128)}) %all-gather.8.cloned.1.call-update) | async-done | bytes 8388624 | tf_op jit(solution)/shard_map/all_gather | solution.py:50
  463.4 31.2 %fusion.6 = f32[1024,512]{1,0:T(8,128)} fusion(f32[1024,512]{1,0:T(8,128)S(1)} %copy-done.9, f32[4096,512]{1,0:T(8,128)} %all-gather.8.cloned.1.call-done, f32[1024,8192]{1,0:T(8,128)} %constant_dynamic-update-slice_fusion, s32[]{:T(128)S(6)} %select_n.14), kind=kOutput, calls=%fused_computation.6 | convolution fusion | flops 25770328064 | bytes 29360132 | tf_op jit(solution)/shard_map/dot_general | solution.py:8
  494.6 58.0 %all-gather.14.cloned.1.call-done = f32[4096,512]{1,0:T(8,128)} async-done(((f32[1024,512]{1,0:T(8,128)}), f32[4096,512]{1,0:T(8,128)}) %all-gather.14.cloned.1.call-update) | async-done | bytes 8388624 | tf_op jit(solution)/shard_map/all_gather | solution.py:52
  552.6 152.6 %all-gather.12.cloned.1.call-done = f32[1024,4096]{1,0:T(8,128)} async-done(((f32[1024,512]{1,0:T(8,128)}), f32[1024,4096]{1,0:T(8,128)}) %all-gather.12.cloned.1.call-update) | async-done | bytes 16777232 | tf_op jit(solution)/shard_map/all_gather | solution.py:51
  705.2 31.0 %fusion.12 = f32[1024,512]{1,0:T(8,128)} fusion(f32[1024,4096]{1,0:T(8,128)} %all-gather.12.cloned.1.call-done, f32[4096,512]{1,0:T(8,128)} %all-gather.14.cloned.1.call-done), kind=kOutput, calls=%fused_computation.26 | convolution fusion | flops 25769803776 | bytes 27262976 | tf_op jit(solution)/shard_map/dot_general | solution.py:8
  (51 shorter events, 27.3 us)
Async XLA Ops:
  7.2 217.4 %copy-start = (f32[1024,512]{1,0:T(8,128)S(1)}, f32[1024,512]{1,0:T(8,128)}, u32[]{:S(2)}) copy-start(f32[1024,512]{1,0:T(8,128)} %param.3) | copy-start | bytes 6291460
  7.2 235.5 %all-gather.6.cloned.1.call-start = ((), (), s32[]{:S(2)}) async-start(), calls=%async_computation.3 | async-start | bytes 10485760 | tf_op jit(solution)/shard_map/all_gather | solution.py:36
  7.2 28.6 %collective-permute-start = (f32[1024,512]{1,0:T(8,128)}, f32[1024,512]{1,0:T(8,128)}, u32[]{:S(2)}, u32[]{:S(2)}) collective-permute-start(f32[1024,512]{1,0:T(8,128)} %param.3), channel_id=1, source_target_pairs={{0,1},{1,2},{2,3},{3,4},{4,5},{5,6},{6,7},{7,0},{8,9},{9,10},{10,1... | collective-permute-start | bytes 6291464 | tf_op jit(solution)/shard_map/ppermute | solution.py:32
  7.9 370.1 %all-gather.10.cloned.1.call-start = ((), (), s32[]{:S(2)}) async-start(), calls=%async_computation.5 | async-start | bytes 10485760 | tf_op jit(solution)/shard_map/all_gather | solution.py:37
  35.8 27.5 %collective-permute-start.1 = (f32[1024,512]{1,0:T(8,128)}, f32[1024,512]{1,0:T(8,128)S(1)}, u32[]{:S(2)}, u32[]{:S(2)}) collective-permute-start(f32[1024,512]{1,0:T(8,128)} %collective-permute-done), channel_id=1, source_target_pairs={{0,1},{1,2},{2,3},{3,4},{4,5},{5,6},{6,7},{7,0},{8,9},{9,10},{10,1... | collective-permute-start | bytes 6291464 | tf_op jit(solution)/shard_map/ppermute | solution.py:32
  63.3 1.4 copy-start.1
  64.7 27.3 %collective-permute-start.2 = (f32[1024,512]{1,0:T(8,128)S(1)}, f32[1024,512]{1,0:T(8,128)S(1)}, u32[]{:S(2)}, u32[]{:S(2)}) collective-permute-start(f32[1024,512]{1,0:T(8,128)S(1)} %collective-permute-done.1), channel_id=1, source_target_pairs={{0,1},{1,2},{2,3},{3,4},{4,5},{5,6},{6,7},{7,0},{8,9},{9,10},{10,1... | collective-permute-start | bytes 6291464 | tf_op jit(solution)/shard_map/ppermute | solution.py:32
  91.9 1.4 copy-start.3
  93.3 27.3 %collective-permute-start.3 = (f32[1024,512]{1,0:T(8,128)S(1)}, f32[1024,512]{1,0:T(8,128)S(1)}, u32[]{:S(2)}, u32[]{:S(2)}) collective-permute-start(f32[1024,512]{1,0:T(8,128)S(1)} %collective-permute-done.2), channel_id=1, source_target_pairs={{0,1},{1,2},{2,3},{3,4},{4,5},{5,6},{6,7},{7,0},{8,9},{9,10},{10,1... | collective-permute-start | bytes 6291464 | tf_op jit(solution)/shard_map/ppermute | solution.py:32
  120.5 1.3 copy-start.5
  121.9 27.3 %collective-permute-start.4 = (f32[1024,512]{1,0:T(8,128)S(1)}, f32[1024,512]{1,0:T(8,128)S(1)}, u32[]{:S(2)}, u32[]{:S(2)}) collective-permute-start(f32[1024,512]{1,0:T(8,128)S(1)} %collective-permute-done.3), channel_id=1, source_target_pairs={{0,1},{1,2},{2,3},{3,4},{4,5},{5,6},{6,7},{7,0},{8,9},{9,10},{10,1... | collective-permute-start | bytes 6291464 | tf_op jit(solution)/shard_map/ppermute | solution.py:32
  149.1 1.3 copy-start.7
  150.4 27.4 %collective-permute-start.5 = (f32[1024,512]{1,0:T(8,128)S(1)}, f32[1024,512]{1,0:T(8,128)}, u32[]{:S(2)}, u32[]{:S(2)}) collective-permute-start(f32[1024,512]{1,0:T(8,128)S(1)} %collective-permute-done.4), channel_id=1, source_target_pairs={{0,1},{1,2},{2,3},{3,4},{4,5},{5,6},{6,7},{7,0},{8,9},{9,10},{10,1... | collective-permute-start | bytes 6291464 | tf_op jit(solution)/shard_map/ppermute | solution.py:32
  177.8 27.6 %collective-permute-start.6 = (f32[1024,512]{1,0:T(8,128)}, f32[1024,512]{1,0:T(8,128)}, u32[]{:S(2)}, u32[]{:S(2)}) collective-permute-start(f32[1024,512]{1,0:T(8,128)} %collective-permute-done.5), channel_id=1, source_target_pairs={{0,1},{1,2},{2,3},{3,4},{4,5},{5,6},{6,7},{7,0},{8,9},{9,10},{10,1... | collective-permute-start | bytes 6291464 | tf_op jit(solution)/shard_map/ppermute | solution.py:32
  177.8 285.6 %all-gather.8.cloned.1.call-start = ((), (), s32[]{:S(2)}) async-start(), calls=%async_computation.4 | async-start | bytes 10485760 | tf_op jit(solution)/shard_map/all_gather | solution.py:50
  177.9 40.1 %copy-start.4 = (f32[1024,512]{1,0:T(8,128)S(1)}, f32[1024,512]{1,0:T(8,128)}, u32[]{:S(2)}) copy-start(f32[1024,512]{1,0:T(8,128)} %copy-done.3) | copy-start | bytes 6291460
  177.9 41.5 %copy-start.2 = (f32[1024,512]{1,0:T(8,128)S(1)}, f32[1024,512]{1,0:T(8,128)}, u32[]{:S(2)}) copy-start(f32[1024,512]{1,0:T(8,128)} %copy-done.1) | copy-start | bytes 6291460
  211.5 20.6 %copy-start.8 = (f32[1024,512]{1,0:T(8,128)S(1)}, f32[1024,512]{1,0:T(8,128)}, u32[]{:S(2)}) copy-start(f32[1024,512]{1,0:T(8,128)} %copy-done.7) | copy-start | bytes 6291460
  214.7 18.9 %copy-start.6 = (f32[1024,512]{1,0:T(8,128)S(1)}, f32[1024,512]{1,0:T(8,128)}, u32[]{:S(2)}) copy-start(f32[1024,512]{1,0:T(8,128)} %copy-done.5) | copy-start | bytes 6291460
  377.8 85.6 %copy-start.9 = (f32[1024,512]{1,0:T(8,128)S(1)}, f32[1024,512]{1,0:T(8,128)}, u32[]{:S(2)}) copy-start(f32[1024,512]{1,0:T(8,128)} %param.5) | copy-start | bytes 6291460
  377.8 174.8 %all-gather.14.cloned.1.call-start = ((), (), s32[]{:S(2)}) async-start(), calls=%async_computation.7 | async-start | bytes 10485760 | tf_op jit(solution)/shard_map/all_gather | solution.py:52
  409.2 295.9 %all-gather.12.cloned.1.call-start = ((), (), s32[]{:S(2)}) async-start(), calls=%async_computation.6 | async-start | bytes 18874368 | tf_op jit(solution)/shard_map/all_gather | solution.py:51
Sparse Core Ops, SparseCore 0:
  9.8 90.1 all-gather.5
  177.9 89.1 all-gather.9
  377.9 85.4 all-gather.7
  465.1 87.4 all-gather.13
  554.1 151.0 all-gather.11
